TPU v7x, 32 devices: a whole 2x2x4 slice. The times are simulated.
32 devices in a mesh: wide: 4 (over y, core), narrow: 4 (over z), depth: 2 (over x).
Axes of the slice: x: 2, y: 2, z: 4, core: 2. Of those that a mesh axis runs over, the one named last changes fastest.
Arguments:
- hidden_state: bfloat16 [16, 4096], P(('wide', 'depth')), may hold values from -6 to 6
- query_weight: bfloat16 [4096, 4096], P('depth', 'narrow'), may hold values from -0.09375 to 0.09375
- output_weight: bfloat16 [4096, 4096], P('narrow'), may hold values from -0.09375 to 0.09375
- cache_keys: bfloat16 [16, 512, 4096], P(('wide', 'depth'), None, 'narrow'), may hold values from -128 to 128
- cache_values: bfloat16 [16, 512, 4096], P(('wide', 'depth'), None, 'narrow'), may hold values from -12 to 12
- enc_blocks: int32 [16], replicated, may hold values from 1 to 4
- cache_slot: int32 [16], replicated, may hold values from 0 to 15, as said below
Outputs:
- attended: bfloat16 [16, 4096], P(('wide', 'depth'), 'narrow')
Inputs may be any that keep to these rules, and one draw needn't show every extreme that they name: Request r attends to the first 128 * enc_blocks[r] rows of its cache slot. Every slot holds exactly one request, and r and cache_slot[r] agree in their value of (index // 2) % 2.
All inputs are finite; a program needn't handle non-finite values.
Results may differ from a plain program's by a relative error of at most 0.012.
The roundings to bfloat16 on the way count: a program that leaves them out, or rounds other values in their place, can miss the bound.
Values may be sent and summed in bfloat16 or wider, within the bound.
No kernel may reach another device: no remote copies, remote signals or barrier semaphores. Data moves between devices by JAX's collectives and lax.ppermute only.
A program may use at most 64 MiB of HBM per device.

v0:
```python
import jax
import jax.numpy as jnp
from jax import lax
from jax.experimental import pallas as pl
from jax.experimental.pallas import tpu as pltpu
from jax.sharding import PartitionSpec as P


HDIM = 64
BLOCK = 128
SUBLANES = 8
LANES = 128

MIB = 1 << 20
VMEM = pl.BlockSpec(memory_space=pltpu.VMEM)
HBM = pl.BlockSpec(memory_space=pltpu.HBM)


def crossing(chip, flip_depth):
    return (chip & 1) ^ flip_depth


def normed_halves(hidden_ref):
    half = hidden_ref.shape[1] // 2
    widened = hidden_ref[...].astype(jnp.float32)
    mean_square = jnp.mean(widened * widened, axis=-1, keepdims=True)
    normed = widened * lax.rsqrt(mean_square + 1e-06)
    low, high = normed[:, :half], normed[:, half:]
    first = lax.axis_index("depth") == 0
    own, other = jnp.where(first, low, high), jnp.where(first, high, low)
    return own.astype(jnp.bfloat16), other.astype(jnp.bfloat16)


def norm_kernel(hidden_ref, own_ref, other_ref):
    own_ref[...], other_ref[...] = normed_halves(hidden_ref)


def arrived_kernel(hidden_ref, own_ref):
    own_ref[...] = normed_halves(hidden_ref)[0]


def wanted_kernel(sizes, wanted_ref):
    halves, rows = sizes
    at_wide, at_depth = lax.axis_index("wide"), lax.axis_index("depth")
    target = lax.broadcasted_iota(jnp.int32, wanted_ref.shape, 0)
    peer = target // rows
    peer_at = (at_wide ^ (peer // 2)) * halves + (at_depth ^ (peer % 2))
    wanted_ref[...] = peer_at * rows + target % rows


def table_kernel(sizes, wanted_ref, slot_hbm, blocks_hbm, place_ref, limit_ref, route_ref, *scratch):
    wide, halves, rows = sizes
    slot_ref, blocks_ref, slot_sem, blocks_sem = scratch
    slot_copy = pltpu.make_async_copy(slot_hbm, slot_ref, slot_sem)
    blocks_copy = pltpu.make_async_copy(blocks_hbm, blocks_ref, blocks_sem)
    slot_copy.start()
    blocks_copy.start()
    slot_copy.wait()
    blocks_copy.wait()
    at_wide, at_depth = lax.axis_index("wide"), lax.axis_index("depth")
    total = slot_ref.shape[1]
    slots = slot_ref[...]

    def iota(count, dim):
        return lax.broadcasted_iota(jnp.int32, (count, total), dim)

    wanted = wanted_ref[...]
    request = jnp.sum(jnp.where(slots == wanted, iota(SUBLANES, 1), 0), axis=1, keepdims=True)
    from_wide = (request // (rows * halves)) ^ at_wide
    from_depth = (request // rows % halves) ^ at_depth
    place = ((from_wide >> 1) * halves + from_depth) * rows + request % rows
    here = (from_wide & 1) == crossing(from_wide >> 1, from_depth)
    place_ref[...] = jnp.broadcast_to(jnp.where(here, place, -1), place_ref.shape)
    base = (at_wide * halves + at_depth) * rows
    for j in range(rows):
        count = jnp.sum(jnp.where(slots == base + j, blocks_ref[...], 0), axis=1, keepdims=True)
        limit_ref[j] = jnp.broadcast_to(count * BLOCK, limit_ref.shape[1:])
    line = iota(wide * rows, 0)
    request = (line // rows * halves + at_depth) * rows + line % rows
    held = jnp.sum(jnp.where(iota(wide * rows, 1) == request, slots, 0), axis=1, keepdims=True)
    route_ref[...] = jnp.broadcast_to(held - base, route_ref.shape)


def turn_kernel(keys_ref, turned_ref):
    for j in range(keys_ref.shape[0]):
        turned_ref[j] = keys_ref[j].T


def query_kernel(rows, order, place_ref, *refs):
    pieces = len(refs) - 1 - 4 - 1
    piece_refs, weight_ref = refs[:pieces], refs[pieces]
    out_refs, rows_ref = refs[pieces + 1 : pieces + 5], refs[pieces + 5]
    for k, piece in zip(order, piece_refs):
        rows_ref[k * rows : (k + 1) * rows, :] = piece[...].astype(jnp.float32)
    sums = jnp.dot(
        rows_ref[...].astype(jnp.bfloat16), weight_ref[...], preferred_element_type=jnp.float32
    )
    place = place_ref[...]
    for c in range(sums.shape[1] // LANES):
        span = slice(c * LANES, (c + 1) * LANES)
        picked = jnp.zeros_like(place, jnp.float32)
        for g in range(sums.shape[0] // SUBLANES):
            lines = sums[g * SUBLANES : (g + 1) * SUBLANES, span]
            found = jnp.take_along_axis(lines, place & (SUBLANES - 1), axis=0)
            picked = jnp.where(place >> 3 == g, found, picked)
        for k, out in enumerate(out_refs):
            out[:, span] = picked[k * rows : (k + 1) * rows]


def attend_kernel(narrow, limit_ref, route_ref, *refs):
    parts, (keys_ref, values_ref, weight_ref, out_ref) = refs[:4], refs[4:]
    rows, features, cache_len = keys_ref.shape
    heads = features // HDIM
    queries = (parts[0][...] + parts[2][...]) + (parts[1][...] + parts[3][...])
    of_head = (
        lax.broadcasted_iota(jnp.int32, (heads, features), 1) // HDIM
        == lax.broadcasted_iota(jnp.int32, (heads, features), 0)
    )
    positions = lax.broadcasted_iota(jnp.int32, (heads, cache_len), 1)
    scores, shares, mixed = [], [], []
    for j in range(rows):
        spread = jnp.where(of_head, queries[j : j + 1, :], 0.0).astype(jnp.bfloat16)
        scores.append(
            jnp.dot(spread, keys_ref[j], preferred_element_type=jnp.float32)
        )
    for j in range(rows):
        masked = jnp.where(positions < limit_ref[j], scores[j], jnp.float32(-1e30))
        row_top = jnp.max(masked, axis=-1, keepdims=True)
        raised = jnp.exp(masked - row_top)
        shares.append((raised / jnp.sum(raised, axis=-1, keepdims=True)).astype(jnp.bfloat16))
    for j in range(rows):
        mixed.append(jnp.dot(shares[j], values_ref[j], preferred_element_type=jnp.float32))
    route = route_ref[...]
    context = jnp.zeros(route.shape, jnp.float32)
    for j in range(rows):
        line = jnp.sum(jnp.where(of_head, mixed[j], 0.0), axis=0, keepdims=True)
        context = jnp.where(route == j, line, context)
    partial = jnp.dot(
        context.astype(jnp.bfloat16), weight_ref[...], preferred_element_type=jnp.float32
    )
    width = partial.shape[1] // narrow
    for to_wide in range(partial.shape[0] // rows):
        block = partial[to_wide * rows : (to_wide + 1) * rows].astype(jnp.bfloat16)
        for to_narrow in range(narrow):
            out_ref[to_wide * narrow + to_narrow] = block[
                :, to_narrow * width : (to_narrow + 1) * width
            ]


def sum_kernel(parts_ref, out_ref):
    total = parts_ref[0].astype(jnp.float32)
    for k in range(1, parts_ref.shape[0]):
        total = total + parts_ref[k].astype(jnp.float32)
    out_ref[...] = total.astype(jnp.bfloat16)


def local_call(kernel, out_shape, count, mib, scratch=(), cost=None, far=0):
    several = isinstance(out_shape, list)
    return pl.pallas_call(
        kernel,
        out_shape=out_shape,
        in_specs=[VMEM] * (count - far) + [HBM] * far,
        out_specs=[VMEM] * len(out_shape) if several else VMEM,
        scratch_shapes=scratch,
        compiler_params=pltpu.CompilerParams(vmem_limit_bytes=mib * MIB),
        cost_estimate=cost,
    )


def cost_of(flops):
    return pl.CostEstimate(flops=flops, bytes_accessed=0, transcendentals=0)


def shards(
    hidden_state, query_weight, output_weight, cache_keys, cache_values, enc_blocks, cache_slot
):
    rows = hidden_state.shape[0]
    wide, narrow, halves = (lax.axis_size(name) for name in ("wide", "narrow", "depth"))
    features = query_weight.shape[1]
    cache_len = cache_keys.shape[1]
    width = output_weight.shape[1]

    def flipped(x, flip_wide, flip_depth):
        pairs = [
            (w * halves + d, (w ^ flip_wide) * halves + (d ^ flip_depth))
            for w in range(wide)
            for d in range(halves)
        ]
        return lax.ppermute(x, ("wide", "depth"), pairs)

    shape = jax.ShapeDtypeStruct
    wanted = local_call(
        lambda *refs: wanted_kernel((halves, rows), *refs),
        shape((4 * rows, cache_slot.shape[0]), jnp.int32),
        0,
        1,
        cost=cost_of(10**10),
    )()
    place, limit, route = local_call(
        lambda *refs: table_kernel((wide, halves, rows), *refs),
        [
            shape((4 * rows, LANES), jnp.int32),
            shape((rows, features // HDIM, cache_len), jnp.int32),
            shape((wide * rows, features), jnp.int32),
        ],
        3,
        1,
        scratch=[
            pltpu.VMEM((1, cache_slot.shape[0]), jnp.int32),
            pltpu.VMEM((1, cache_slot.shape[0]), jnp.int32),
            pltpu.SemaphoreType.DMA(()),
            pltpu.SemaphoreType.DMA(()),
        ],
        cost=cost_of(10**9),
        far=2,
    )(wanted, cache_slot[None], enc_blocks[None])
    half_rows = shape((rows, query_weight.shape[0]), jnp.bfloat16)
    own, other = local_call(
        norm_kernel, [half_rows, half_rows], 1, 1, cost=cost_of(5 * 10**9)
    )(hidden_state)
    turned = local_call(
        turn_kernel,
        shape((rows, features, cache_len), jnp.bfloat16),
        1,
        6,
    )(cache_keys)
    pieces, order = [own], [0]
    last = wide // 2 * halves - 1
    for k in range(1, last + 1):
        chip, flip_depth = k // halves, k % halves
        flip_wide = chip * 2 + crossing(chip, flip_depth)
        if k == last:
            raw = flipped(hidden_state, flip_wide, flip_depth)
            piece = local_call(arrived_kernel, half_rows, 1, 1)(raw)
        else:
            piece = flipped(other if flip_depth else own, flip_wide, flip_depth)
        pieces.append(piece)
        order.append(k)
    parts = local_call(
        lambda *refs: query_kernel(rows, order, *refs),
        [shape((rows, features), jnp.float32)] * 4,
        len(pieces) + 2,
        6,
        scratch=[pltpu.VMEM((len(pieces) * rows, query_weight.shape[0]), jnp.float32)],
    )(place, *pieces, query_weight)
    arrived = [parts[0]] + [flipped(parts[k], k // 2, k % 2) for k in (1, 3, 2)]
    spread = local_call(
        lambda *refs: attend_kernel(narrow, *refs),
        shape((wide * narrow, rows, width // narrow), jnp.bfloat16),
        9,
        16,
    )(limit, route, *arrived, turned, cache_values, output_weight)
    gathered = lax.all_to_all(spread, ("wide", "narrow"), 0, 0, tiled=True)
    return local_call(
        sum_kernel, shape((rows, width // narrow), jnp.bfloat16), 1, 1
    )(gathered)


def solution(mesh):
    placed = (
        P(("wide", "depth"), None),
        P("depth", "narrow"),
        P("narrow", None),
        P(("wide", "depth"), None, "narrow"),
        P(("wide", "depth"), None, "narrow"),
        P(),
        P(),
    )
    return jax.shard_map(
        shards,
        mesh=mesh,
        in_specs=placed,
        out_specs=P(("wide", "depth"), "narrow"),
        check_vma=False,
    )
```

profile of v0, /device:TPU:0, one launch (start us, length us, event | category | flops | bytes accessed | tf_op | source)
XLA Modules:
  0.0 28.0 jit_solution(9293517272677416456)
XLA Ops:
  0.0 3.9 %collective-permute-start.2 = (bf16[2,4096]{1,0:T(2,128)(2,1)}, bf16[2,4096]{1,0:T(2,128)(2,1)S(1)}, u32[]{:S(2)}, u32[]{:S(2)}) collective-permute-start(bf16[2,4096]{1,0:T(2,128)(2,1)} %hidden_ref.1), channel_id=1, source_target_pairs={{0,17},{1,16},{8,25},{9,24},{16,1},{17,0},{24,9},{25,8},{2,19},{3,... | collective-permute-start | bytes 49160 | tf_op jit(solution)/shard_map/ppermute | solution.py:189
  3.9 0.0 copy-start.3
  3.9 0.7 %copy-done.3 = bf16[2,4096]{1,0:T(2,128)(2,1)S(1)} copy-done((bf16[2,4096]{1,0:T(2,128)(2,1)S(1)}, bf16[2,4096]{1,0:T(2,128)(2,1)}, u32[]{:S(2)}) %copy-start.3) | copy-done | bytes 16408
  4.7 0.1 shard_map.75
  4.8 0.1 collective-permute-start
  4.9 0.0 copy-start.4
  4.9 0.0 copy-start.5
  4.9 0.0 slice-start.1
  4.9 0.2 collective-permute-start.1
  5.2 0.5 %copy-done.4 = s32[16]{0:T(128)S(1)} copy-done((s32[16]{0:T(128)S(1)}, s32[16]{0:T(128)}, u32[]{:S(2)}) %copy-start.4) | copy-done | bytes 88
  5.7 0.0 copy-done.5
  5.7 0.1 shard_map.74
  5.9 0.0 collective-permute-done.2.hidden_ref
  5.9 0.1 shard_map.76.refs_4_
  6.0 2.0 %collective-permute-done.refs_2_ = bf16[2,2048]{1,0:T(2,128)(2,1)S(1)} collective-permute-done((bf16[2,2048]{1,0:T(2,128)(2,1)S(1)}, bf16[2,2048]{1,0:T(2,128)(2,1)S(1)}, u32[]{:S(2)}, u32[]{:S(2)}) %collective-permute-start) | collective-permute-done | bytes 8224 | tf_op jit(solution)/shard_map/ppermute | solution.py:189
  8.0 0.1 collective-permute-done.1.refs_3_
  8.1 0.0 copy-done
  8.1 0.7 %shard_map.77 = (f32[2,1024]{1,0:T(2,128)S(1)}, f32[2,1024]{1,0:T(2,128)S(1)}, f32[2,1024]{1,0:T(2,128)S(1)}, f32[2,1024]{1,0:T(2,128)S(1)}) custom-call(s32[8,128]{1,0:T(8,128)S(1)} %get-tuple-element.16.refs_0_, bf16[2,2048]{1,0:T(2,128)(2,1)S(1)} %get-tuple-element.17.refs_1_, bf16[2,2048]{1,0:T(2,128)(2,1)S(1)} %collective-permute-done.refs_2_, ...), custom_call_target="tpu_custom_call" | custom-call | tf_op jit(solution)/shard_map/pallas_call | solution.py:239
  8.7 1.5 %collective-permute-start.3 = (f32[2,1024]{1,0:T(2,128)S(1)}, f32[2,1024]{1,0:T(2,128)S(1)}, u32[]{:S(2)}, u32[]{:S(2)}) collective-permute-start(f32[2,1024]{1,0:T(2,128)S(1)} %get-tuple-element.20), channel_id=1, source_target_pairs={{0,1},{1,0},{8,9},{9,8},{16,17},{17,16},{24,25},{25,24},{2,3},{3,2... | collective-permute-start | bytes 24584 | tf_op jit(solution)/shard_map/ppermute | solution.py:189
  10.3 0.4 %collective-permute-start.4 = (f32[2,1024]{1,0:T(2,128)S(1)}, f32[2,1024]{1,0:T(2,128)S(1)}, u32[]{:S(2)}, u32[]{:S(2)}) collective-permute-start(f32[2,1024]{1,0:T(2,128)S(1)} %get-tuple-element.21), channel_id=1, source_target_pairs={{0,9},{1,8},{8,1},{9,0},{16,25},{17,24},{24,17},{25,16},{2,11},{3,... | collective-permute-start | bytes 24584 | tf_op jit(solution)/shard_map/ppermute | solution.py:189
  10.6 0.2 collective-permute-start.5
  10.9 0.0 copy-done.2
  10.9 0.6 %shard_map.78.refs_6_ = bf16[2,1024,512]{2,1,0:T(8,128)(2,1)S(1)} custom-call(bf16[2,512,1024]{2,1,0:T(8,128)(2,1)S(1)} %copy-done.2), custom_call_target="tpu_custom_call" | custom-call | tf_op jit(solution)/shard_map/pallas_call | solution.py:221
  11.5 0.9 %collective-permute-done.3.refs_3_ = f32[2,1024]{1,0:T(2,128)S(1)} collective-permute-done((f32[2,1024]{1,0:T(2,128)S(1)}, f32[2,1024]{1,0:T(2,128)S(1)}, u32[]{:S(2)}, u32[]{:S(2)}) %collective-permute-start.3) | collective-permute-done | bytes 8224 | tf_op jit(solution)/shard_map/ppermute | solution.py:189
  12.4 0.9 %collective-permute-done.4.refs_4_ = f32[2,1024]{1,0:T(2,128)S(1)} collective-permute-done((f32[2,1024]{1,0:T(2,128)S(1)}, f32[2,1024]{1,0:T(2,128)S(1)}, u32[]{:S(2)}, u32[]{:S(2)}) %collective-permute-start.4) | collective-permute-done | bytes 8224 | tf_op jit(solution)/shard_map/ppermute | solution.py:189
  13.3 0.0 collective-permute-done.5.refs_5_
  13.3 0.0 slice-done
  13.4 0.0 slice-done.1
  13.4 0.0 copy-done.1
  13.4 1.9 %shard_map.79 = bf16[16,2,1024]{2,1,0:T(2,128)(2,1)S(1)} custom-call(s32[2,16,512]{2,1,0:T(8,128)S(1)} %get-tuple-element.14.refs_0_, s32[8,1024]{1,0:T(8,128)S(1)} %get-tuple-element.15.refs_1_, f32[2,1024]{1,0:T(2,128)S(1)} %get-tuple-element.19.refs_2_, f32[2,1024]{1,0:T(2,128)S(1)} %collective-permute-done.3.refs_3_, ...), custom_call_target="tpu_custom_call" | custom-call | tf_op jit(solution)/shard_map/pallas_call | solution.py:247
  15.3 12.1 %all_to_all.5.parts_ref = bf16[16,2,1024]{2,1,0:T(2,128)(2,1)S(1)} all-to-all(bf16[16,2,1024]{2,1,0:T(2,128)(2,1)S(1)} %shard_map.79), channel_id=1, replica_groups=mesh['wide'=4,'narrow'=4,'depth'=2] {'wide','narrow'}, dimensions={0} | all-to-all | bytes 131072 | tf_op jit(solution)/shard_map/all_to_all | solution.py:253
  27.4 0.6 %shard_map.80 = bf16[2,1024]{1,0:T(2,128)(2,1)} custom-call(bf16[16,2,1024]{2,1,0:T(2,128)(2,1)S(1)} %all_to_all.5.parts_ref), custom_call_target="tpu_custom_call" | custom-call | tf_op jit(solution)/shard_map/pallas_call | solution.py:254
  (6 shorter events, 0.0 us)
Async XLA Ops:
  0.0 5.9 %collective-permute-start.2 = (bf16[2,4096]{1,0:T(2,128)(2,1)}, bf16[2,4096]{1,0:T(2,128)(2,1)S(1)}, u32[]{:S(2)}, u32[]{:S(2)}) collective-permute-start(bf16[2,4096]{1,0:T(2,128)(2,1)} %hidden_ref.1), channel_id=1, source_target_pairs={{0,17},{1,16},{8,25},{9,24},{16,1},{17,0},{24,9},{25,8},{2,19},{3,... | collective-permute-start | bytes 49160 | tf_op jit(solution)/shard_map/ppermute | solution.py:189
  3.9 0.8 %copy-start.3 = (bf16[2,4096]{1,0:T(2,128)(2,1)S(1)}, bf16[2,4096]{1,0:T(2,128)(2,1)}, u32[]{:S(2)}) copy-start(bf16[2,4096]{1,0:T(2,128)(2,1)} %hidden_ref.1) | copy-start | bytes 49156
  4.7 8.7 %slice-start = ((s8[8388608]{0:T(1024)(128)(4,1)}), s8[4194304]{0:T(1024)(128)(4,1)S(1)}, s32[]{:S(2)}) async-start(s8[8388608]{0:T(1024)(128)(4,1)} %bitcast.2), calls=%async_computation.1 | async-start | bytes 8388608
  4.8 3.1 %collective-permute-start = (bf16[2,2048]{1,0:T(2,128)(2,1)S(1)}, bf16[2,2048]{1,0:T(2,128)(2,1)S(1)}, u32[]{:S(2)}, u32[]{:S(2)}) collective-permute-start(bf16[2,2048]{1,0:T(2,128)(2,1)S(1)} %get-tuple-element.18), channel_id=1, source_target_pairs={{0,9},{1,8},{8,1},{9,0},{16,25},{17,24},{24,17},{25,16},{2,11},{3,... | collective-permute-start | bytes 24584 | tf_op jit(solution)/shard_map/ppermute | solution.py:189
  4.9 0.8 %copy-start.4 = (s32[16]{0:T(128)S(1)}, s32[16]{0:T(128)}, u32[]{:S(2)}) copy-start(s32[16]{0:T(128)} %param.13) | copy-start | bytes 196
  4.9 0.8 %copy-start.5 = (s32[16]{0:T(128)S(1)}, s32[16]{0:T(128)}, u32[]{:S(2)}) copy-start(s32[16]{0:T(128)} %param.12) | copy-start | bytes 196
  4.9 8.4 %slice-start.1 = ((s8[8388608]{0:T(1024)(128)(4,1)}), s8[4194304]{0:T(1024)(128)(4,1)S(1)}, s32[]{:S(2)}) async-start(s8[8388608]{0:T(1024)(128)(4,1)} %bitcast.2), calls=%async_computation.2 | async-start | bytes 8388608
  4.9 3.1 %collective-permute-start.1 = (bf16[2,2048]{1,0:T(2,128)(2,1)S(1)}, bf16[2,2048]{1,0:T(2,128)(2,1)S(1)}, u32[]{:S(2)}, u32[]{:S(2)}) collective-permute-start(bf16[2,2048]{1,0:T(2,128)(2,1)S(1)} %get-tuple-element.17.refs_1_), channel_id=1, source_target_pairs={{0,24},{1,25},{8,16},{9,17},{16,8},{17,9},{24,0},{25,1},{2,26},{3,... | collective-permute-start | bytes 24584 | tf_op jit(solution)/shard_map/ppermute | solution.py:189
  5.2 2.9 %copy-start = (bf16[2048,1024]{1,0:T(8,128)(2,1)S(1)}, bf16[2048,1024]{1,0:T(8,128)(2,1)}, u32[]{:S(2)}) copy-start(bf16[2048,1024]{1,0:T(8,128)(2,1)} %refs_5_.1) | copy-start | bytes 12582916
  8.1 2.8 %copy-start.2 = (bf16[2,512,1024]{2,1,0:T(8,128)(2,1)S(1)}, bf16[2,512,1024]{2,1,0:T(8,128)(2,1)}, u32[]{:S(2)}) copy-start(bf16[2,512,1024]{2,1,0:T(8,128)(2,1)} %keys_ref.1) | copy-start | bytes 6291460
  8.7 3.7 %collective-permute-start.3 = (f32[2,1024]{1,0:T(2,128)S(1)}, f32[2,1024]{1,0:T(2,128)S(1)}, u32[]{:S(2)}, u32[]{:S(2)}) collective-permute-start(f32[2,1024]{1,0:T(2,128)S(1)} %get-tuple-element.20), channel_id=1, source_target_pairs={{0,1},{1,0},{8,9},{9,8},{16,17},{17,16},{24,25},{25,24},{2,3},{3,2... | collective-permute-start | bytes 24584 | tf_op jit(solution)/shard_map/ppermute | solution.py:189
  10.3 3.1 %collective-permute-start.4 = (f32[2,1024]{1,0:T(2,128)S(1)}, f32[2,1024]{1,0:T(2,128)S(1)}, u32[]{:S(2)}, u32[]{:S(2)}) collective-permute-start(f32[2,1024]{1,0:T(2,128)S(1)} %get-tuple-element.21), channel_id=1, source_target_pairs={{0,9},{1,8},{8,1},{9,0},{16,25},{17,24},{24,17},{25,16},{2,11},{3,... | collective-permute-start | bytes 24584 | tf_op jit(solution)/shard_map/ppermute | solution.py:189
  10.6 2.7 %copy-start.1 = (bf16[2,512,1024]{2,1,0:T(8,128)(2,1)S(1)}, bf16[2,512,1024]{2,1,0:T(8,128)(2,1)}, u32[]{:S(2)}) copy-start(bf16[2,512,1024]{2,1,0:T(8,128)(2,1)} %refs_7_.1) | copy-start | bytes 6291460
  10.6 2.7 %collective-permute-start.5 = (f32[2,1024]{1,0:T(2,128)S(1)}, f32[2,1024]{1,0:T(2,128)S(1)}, u32[]{:S(2)}, u32[]{:S(2)}) collective-permute-start(f32[2,1024]{1,0:T(2,128)S(1)} %get-tuple-element.22), channel_id=1, source_target_pairs={{0,8},{1,9},{8,0},{9,1},{16,24},{17,25},{24,16},{25,17},{2,10},{3,... | collective-permute-start | bytes 24584 | tf_op jit(solution)/shard_map/ppermute | solution.py:189
where the time goes:
time: 28.2 us; the launch traced here: 28 us
  blocking collectives  12.1 us (43%)
  starting transfers between devices  6.38 us (23%)
  Pallas kernels  4.18 us (15%)
  waiting for transfers between devices  3.92 us (14%)
  local copies, waits for them, and re-layouts  1.3 us (5%)
    all_to_all x1, blocking collectives, shards(): gathered = lax.all_to_all(spread, ('wide', 'narrow'), 0, 0, tiled=True)  12.1 us
    ppermute x6, starting transfers between devices, flipped(): return lax.ppermute(x, ('wide', 'depth'), pairs)  6.38 us
    ppermute x6, waiting for transfers between devices, flipped(): return lax.ppermute(x, ('wide', 'depth'), pairs)  3.92 us
    pallas_call x1, Pallas kernels, shards(): local_call(lambda *refs: attend_kernel(narrow, *refs), shape((wide * narr...  1.89 us
    unnamed x16, local copies, waits for them, and re-layouts  1.3 us
    pallas_call x1, Pallas kernels, shards(): local_call(lambda *refs: query_kernel(rows, order, *refs), [shape((rows,...  0.66 us
    pallas_call x1, Pallas kernels, shards(): local_call(sum_kernel, shape((rows, width // narrow), jnp.bfloat16), 1, 1)  0.62 us
    pallas_call x1, Pallas kernels, shards(): local_call(turn_kernel, shape((rows, features, cache_len), jnp.bfloat16),...  0.59 us
  transfers between devices with their start and end apart: 6, of which 4 were waited for; matrix products, arithmetic and copies ran while one was open for 0% of the time, Pallas kernels for 4%

commit v1 on v0

--- a/solution.py
+++ b/solution.py
@@ -135,16 +135,14 @@
     for j in range(rows):
         line = jnp.sum(jnp.where(of_head, mixed[j], 0.0), axis=0, keepdims=True)
         context = jnp.where(route == j, line, context)
-    partial = jnp.dot(
-        context.astype(jnp.bfloat16), weight_ref[...], preferred_element_type=jnp.float32
-    )
-    width = partial.shape[1] // narrow
-    for to_wide in range(partial.shape[0] // rows):
-        block = partial[to_wide * rows : (to_wide + 1) * rows].astype(jnp.bfloat16)
-        for to_narrow in range(narrow):
-            out_ref[to_wide * narrow + to_narrow] = block[
-                :, to_narrow * width : (to_narrow + 1) * width
-            ]
+    context = context.astype(jnp.bfloat16)
+    width = weight_ref.shape[1] // narrow
+    for to_narrow in range(narrow):
+        span = slice(to_narrow * width, (to_narrow + 1) * width)
+        partial = jnp.dot(context, weight_ref[:, span], preferred_element_type=jnp.float32)
+        for to_wide in range(partial.shape[0] // rows):
+            block = partial[to_wide * rows : (to_wide + 1) * rows]
+            out_ref[to_wide * narrow + to_narrow] = block.astype(jnp.bfloat16)
 
 
 def sum_kernel(parts_ref, out_ref):

time: 28.2 us -> 28.2 us (level)
  no operation moved by 1% of the time
where the time goes in v1:
time: 28.2 us; the launch traced here: 28 us
  blocking collectives  12.1 us (43%)
  starting transfers between devices  6.38 us (23%)
  Pallas kernels  4.18 us (15%)
  waiting for transfers between devices  3.92 us (14%)
  local copies, waits for them, and re-layouts  1.3 us (5%)
    all_to_all x1, blocking collectives, shards(): gathered = lax.all_to_all(spread, ('wide', 'narrow'), 0, 0, tiled=True)  12.1 us
    ppermute x6, starting transfers between devices, flipped(): return lax.ppermute(x, ('wide', 'depth'), pairs)  6.38 us
    ppermute x6, waiting for transfers between devices, flipped(): return lax.ppermute(x, ('wide', 'depth'), pairs)  3.92 us
    pallas_call x1, Pallas kernels, shards(): local_call(lambda *refs: attend_kernel(narrow, *refs), shape((wide * narr...  1.89 us
    unnamed x16, local copies, waits for them, and re-layouts  1.3 us
    pallas_call x1, Pallas kernels, shards(): local_call(lambda *refs: query_kernel(rows, order, *refs), [shape((rows,...  0.66 us
    pallas_call x1, Pallas kernels, shards(): local_call(sum_kernel, shape((rows, width // narrow), jnp.bfloat16), 1, 1)  0.62 us
    pallas_call x1, Pallas kernels, shards(): local_call(turn_kernel, shape((rows, features, cache_len), jnp.bfloat16),...  0.59 us
  transfers between devices with their start and end apart: 6, of which 4 were waited for; matrix products, arithmetic and copies ran while one was open for 0% of the time, Pallas kernels for 4%

profile of v1, /device:TPU:0, one launch (start us, length us, event | category | flops | bytes accessed | tf_op | source)
XLA Modules:
  0.0 28.0 jit_solution(9293517272677416456)
XLA Ops:
  0.0 3.9 %collective-permute-start.2 = (bf16[2,4096]{1,0:T(2,128)(2,1)}, bf16[2,4096]{1,0:T(2,128)(2,1)S(1)}, u32[]{:S(2)}, u32[]{:S(2)}) collective-permute-start(bf16[2,4096]{1,0:T(2,128)(2,1)} %hidden_ref.1), channel_id=1, source_target_pairs={{0,17},{1,16},{8,25},{9,24},{16,1},{17,0},{24,9},{25,8},{2,19},{3,... | collective-permute-start | bytes 49160 | tf_op jit(solution)/shard_map/ppermute | solution.py:187
  3.9 0.0 copy-start.3
  3.9 0.7 %copy-done.3 = bf16[2,4096]{1,0:T(2,128)(2,1)S(1)} copy-done((bf16[2,4096]{1,0:T(2,128)(2,1)S(1)}, bf16[2,4096]{1,0:T(2,128)(2,1)}, u32[]{:S(2)}) %copy-start.3) | copy-done | bytes 16408
  4.7 0.1 shard_map.75
  4.8 0.1 collective-permute-start
  4.9 0.0 copy-start.4
  4.9 0.0 copy-start.5
  4.9 0.0 slice-start.1
  4.9 0.2 collective-permute-start.1
  5.2 0.5 %copy-done.4 = s32[16]{0:T(128)S(1)} copy-done((s32[16]{0:T(128)S(1)}, s32[16]{0:T(128)}, u32[]{:S(2)}) %copy-start.4) | copy-done | bytes 88
  5.7 0.0 copy-done.5
  5.7 0.1 shard_map.74
  5.9 0.0 collective-permute-done.2.hidden_ref
  5.9 0.1 shard_map.76.refs_4_
  6.0 2.0 %collective-permute-done.refs_2_ = bf16[2,2048]{1,0:T(2,128)(2,1)S(1)} collective-permute-done((bf16[2,2048]{1,0:T(2,128)(2,1)S(1)}, bf16[2,2048]{1,0:T(2,128)(2,1)S(1)}, u32[]{:S(2)}, u32[]{:S(2)}) %collective-permute-start) | collective-permute-done | bytes 8224 | tf_op jit(solution)/shard_map/ppermute | solution.py:187
  8.0 0.1 collective-permute-done.1.refs_3_
  8.1 0.0 copy-done
  8.1 0.7 %shard_map.77 = (f32[2,1024]{1,0:T(2,128)S(1)}, f32[2,1024]{1,0:T(2,128)S(1)}, f32[2,1024]{1,0:T(2,128)S(1)}, f32[2,1024]{1,0:T(2,128)S(1)}) custom-call(s32[8,128]{1,0:T(8,128)S(1)} %get-tuple-element.16.refs_0_, bf16[2,2048]{1,0:T(2,128)(2,1)S(1)} %get-tuple-element.17.refs_1_, bf16[2,2048]{1,0:T(2,128)(2,1)S(1)} %collective-permute-done.refs_2_, ...), custom_call_target="tpu_custom_call" | custom-call | tf_op jit(solution)/shard_map/pallas_call | solution.py:237
  8.7 1.5 %collective-permute-start.3 = (f32[2,1024]{1,0:T(2,128)S(1)}, f32[2,1024]{1,0:T(2,128)S(1)}, u32[]{:S(2)}, u32[]{:S(2)}) collective-permute-start(f32[2,1024]{1,0:T(2,128)S(1)} %get-tuple-element.20), channel_id=1, source_target_pairs={{0,1},{1,0},{8,9},{9,8},{16,17},{17,16},{24,25},{25,24},{2,3},{3,2... | collective-permute-start | bytes 24584 | tf_op jit(solution)/shard_map/ppermute | solution.py:187
  10.3 0.4 %collective-permute-start.4 = (f32[2,1024]{1,0:T(2,128)S(1)}, f32[2,1024]{1,0:T(2,128)S(1)}, u32[]{:S(2)}, u32[]{:S(2)}) collective-permute-start(f32[2,1024]{1,0:T(2,128)S(1)} %get-tuple-element.21), channel_id=1, source_target_pairs={{0,9},{1,8},{8,1},{9,0},{16,25},{17,24},{24,17},{25,16},{2,11},{3,... | collective-permute-start | bytes 24584 | tf_op jit(solution)/shard_map/ppermute | solution.py:187
  10.6 0.2 collective-permute-start.5
  10.9 0.0 copy-done.2
  10.9 0.6 %shard_map.78.refs_6_ = bf16[2,1024,512]{2,1,0:T(8,128)(2,1)S(1)} custom-call(bf16[2,512,1024]{2,1,0:T(8,128)(2,1)S(1)} %copy-done.2), custom_call_target="tpu_custom_call" | custom-call | tf_op jit(solution)/shard_map/pallas_call | solution.py:219
  11.5 0.9 %collective-permute-done.3.refs_3_ = f32[2,1024]{1,0:T(2,128)S(1)} collective-permute-done((f32[2,1024]{1,0:T(2,128)S(1)}, f32[2,1024]{1,0:T(2,128)S(1)}, u32[]{:S(2)}, u32[]{:S(2)}) %collective-permute-start.3) | collective-permute-done | bytes 8224 | tf_op jit(solution)/shard_map/ppermute | solution.py:187
  12.4 0.9 %collective-permute-done.4.refs_4_ = f32[2,1024]{1,0:T(2,128)S(1)} collective-permute-done((f32[2,1024]{1,0:T(2,128)S(1)}, f32[2,1024]{1,0:T(2,128)S(1)}, u32[]{:S(2)}, u32[]{:S(2)}) %collective-permute-start.4) | collective-permute-done | bytes 8224 | tf_op jit(solution)/shard_map/ppermute | solution.py:187
  13.3 0.0 collective-permute-done.5.refs_5_
  13.3 0.0 slice-done
  13.4 0.0 slice-done.1
  13.4 0.0 copy-done.1
  13.4 1.9 %shard_map.79 = bf16[16,2,1024]{2,1,0:T(2,128)(2,1)S(1)} custom-call(s32[2,16,512]{2,1,0:T(8,128)S(1)} %get-tuple-element.14.refs_0_, s32[8,1024]{1,0:T(8,128)S(1)} %get-tuple-element.15.refs_1_, f32[2,1024]{1,0:T(2,128)S(1)} %get-tuple-element.19.refs_2_, f32[2,1024]{1,0:T(2,128)S(1)} %collective-permute-done.3.refs_3_, ...), custom_call_target="tpu_custom_call" | custom-call | tf_op jit(solution)/shard_map/pallas_call | solution.py:245
  15.3 12.1 %all_to_all.5.parts_ref = bf16[16,2,1024]{2,1,0:T(2,128)(2,1)S(1)} all-to-all(bf16[16,2,1024]{2,1,0:T(2,128)(2,1)S(1)} %shard_map.79), channel_id=1, replica_groups=mesh['wide'=4,'narrow'=4,'depth'=2] {'wide','narrow'}, dimensions={0} | all-to-all | bytes 131072 | tf_op jit(solution)/shard_map/all_to_all | solution.py:251
  27.4 0.6 %shard_map.80 = bf16[2,1024]{1,0:T(2,128)(2,1)} custom-call(bf16[16,2,1024]{2,1,0:T(2,128)(2,1)S(1)} %all_to_all.5.parts_ref), custom_call_target="tpu_custom_call" | custom-call | tf_op jit(solution)/shard_map/pallas_call | solution.py:252
  (6 shorter events, 0.0 us)
Async XLA Ops:
  0.0 5.9 %collective-permute-start.2 = (bf16[2,4096]{1,0:T(2,128)(2,1)}, bf16[2,4096]{1,0:T(2,128)(2,1)S(1)}, u32[]{:S(2)}, u32[]{:S(2)}) collective-permute-start(bf16[2,4096]{1,0:T(2,128)(2,1)} %hidden_ref.1), channel_id=1, source_target_pairs={{0,17},{1,16},{8,25},{9,24},{16,1},{17,0},{24,9},{25,8},{2,19},{3,... | collective-permute-start | bytes 49160 | tf_op jit(solution)/shard_map/ppermute | solution.py:187
  3.9 0.8 %copy-start.3 = (bf16[2,4096]{1,0:T(2,128)(2,1)S(1)}, bf16[2,4096]{1,0:T(2,128)(2,1)}, u32[]{:S(2)}) copy-start(bf16[2,4096]{1,0:T(2,128)(2,1)} %hidden_ref.1) | copy-start | bytes 49156
  4.7 8.7 %slice-start = ((s8[8388608]{0:T(1024)(128)(4,1)}), s8[4194304]{0:T(1024)(128)(4,1)S(1)}, s32[]{:S(2)}) async-start(s8[8388608]{0:T(1024)(128)(4,1)} %bitcast.2), calls=%async_computation.1 | async-start | bytes 8388608
  4.8 3.1 %collective-permute-start = (bf16[2,2048]{1,0:T(2,128)(2,1)S(1)}, bf16[2,2048]{1,0:T(2,128)(2,1)S(1)}, u32[]{:S(2)}, u32[]{:S(2)}) collective-permute-start(bf16[2,2048]{1,0:T(2,128)(2,1)S(1)} %get-tuple-element.18), channel_id=1, source_target_pairs={{0,9},{1,8},{8,1},{9,0},{16,25},{17,24},{24,17},{25,16},{2,11},{3,... | collective-permute-start | bytes 24584 | tf_op jit(solution)/shard_map/ppermute | solution.py:187
  4.9 0.8 %copy-start.4 = (s32[16]{0:T(128)S(1)}, s32[16]{0:T(128)}, u32[]{:S(2)}) copy-start(s32[16]{0:T(128)} %param.13) | copy-start | bytes 196
  4.9 0.8 %copy-start.5 = (s32[16]{0:T(128)S(1)}, s32[16]{0:T(128)}, u32[]{:S(2)}) copy-start(s32[16]{0:T(128)} %param.12) | copy-start | bytes 196
  4.9 8.4 %slice-start.1 = ((s8[8388608]{0:T(1024)(128)(4,1)}), s8[4194304]{0:T(1024)(128)(4,1)S(1)}, s32[]{:S(2)}) async-start(s8[8388608]{0:T(1024)(128)(4,1)} %bitcast.2), calls=%async_computation.2 | async-start | bytes 8388608
  4.9 3.1 %collective-permute-start.1 = (bf16[2,2048]{1,0:T(2,128)(2,1)S(1)}, bf16[2,2048]{1,0:T(2,128)(2,1)S(1)}, u32[]{:S(2)}, u32[]{:S(2)}) collective-permute-start(bf16[2,2048]{1,0:T(2,128)(2,1)S(1)} %get-tuple-element.17.refs_1_), channel_id=1, source_target_pairs={{0,24},{1,25},{8,16},{9,17},{16,8},{17,9},{24,0},{25,1},{2,26},{3,... | collective-permute-start | bytes 24584 | tf_op jit(solution)/shard_map/ppermute | solution.py:187
  5.2 2.9 %copy-start = (bf16[2048,1024]{1,0:T(8,128)(2,1)S(1)}, bf16[2048,1024]{1,0:T(8,128)(2,1)}, u32[]{:S(2)}) copy-start(bf16[2048,1024]{1,0:T(8,128)(2,1)} %refs_5_.1) | copy-start | bytes 12582916
  8.1 2.8 %copy-start.2 = (bf16[2,512,1024]{2,1,0:T(8,128)(2,1)S(1)}, bf16[2,512,1024]{2,1,0:T(8,128)(2,1)}, u32[]{:S(2)}) copy-start(bf16[2,512,1024]{2,1,0:T(8,128)(2,1)} %keys_ref.1) | copy-start | bytes 6291460
  8.7 3.7 %collective-permute-start.3 = (f32[2,1024]{1,0:T(2,128)S(1)}, f32[2,1024]{1,0:T(2,128)S(1)}, u32[]{:S(2)}, u32[]{:S(2)}) collective-permute-start(f32[2,1024]{1,0:T(2,128)S(1)} %get-tuple-element.20), channel_id=1, source_target_pairs={{0,1},{1,0},{8,9},{9,8},{16,17},{17,16},{24,25},{25,24},{2,3},{3,2... | collective-permute-start | bytes 24584 | tf_op jit(solution)/shard_map/ppermute | solution.py:187
  10.3 3.1 %collective-permute-start.4 = (f32[2,1024]{1,0:T(2,128)S(1)}, f32[2,1024]{1,0:T(2,128)S(1)}, u32[]{:S(2)}, u32[]{:S(2)}) collective-permute-start(f32[2,1024]{1,0:T(2,128)S(1)} %get-tuple-element.21), channel_id=1, source_target_pairs={{0,9},{1,8},{8,1},{9,0},{16,25},{17,24},{24,17},{25,16},{2,11},{3,... | collective-permute-start | bytes 24584 | tf_op jit(solution)/shard_map/ppermute | solution.py:187
  10.6 2.7 %copy-start.1 = (bf16[2,512,1024]{2,1,0:T(8,128)(2,1)S(1)}, bf16[2,512,1024]{2,1,0:T(8,128)(2,1)}, u32[]{:S(2)}) copy-start(bf16[2,512,1024]{2,1,0:T(8,128)(2,1)} %refs_7_.1) | copy-start | bytes 6291460
  10.6 2.7 %collective-permute-start.5 = (f32[2,1024]{1,0:T(2,128)S(1)}, f32[2,1024]{1,0:T(2,128)S(1)}, u32[]{:S(2)}, u32[]{:S(2)}) collective-permute-start(f32[2,1024]{1,0:T(2,128)S(1)} %get-tuple-element.22), channel_id=1, source_target_pairs={{0,8},{1,9},{8,0},{9,1},{16,24},{17,25},{24,16},{25,17},{2,10},{3,... | collective-permute-start | bytes 24584 | tf_op jit(solution)/shard_map/ppermute | solution.py:187
